TPU v7x, 32 devices: a whole 2x2x4 slice. The times are simulated.
32 devices in a mesh: ty: 4 (over z), tx: 8 (over y, x, core).
Axes of the slice: x: 2, y: 2, z: 4, core: 2. Of those that a mesh axis runs over, the one named last changes fastest.
Arguments:
- object_slices: float32 [2, 2, 2048, 4096], P(None, None, 'ty', 'tx'), may hold values from -4 to 4
- probe_modes: float32 [4, 2, 128, 128], replicated, may hold values from -12 to 12
- patterns: bfloat16 [256, 128, 128], P(('ty', 'tx')), may hold values from 0 to 2
- positions: int32 [256, 2], replicated, may hold values from 0 to 4095, as said below
- counts: int32 [32], replicated, may hold values from 6 to 8, as said below
Outputs:
- new_object: float32 [2, 2, 2048, 4096], P(None, None, 'ty', 'tx')
- new_probe: float32 [4, 2, 128, 128], replicated
Inputs may be any that keep to these rules, and one draw needn't show every extreme that they name: positions[j] is the centre of pattern j, which was acquired by device j // 8 of ty+tx (ty slowest); its column lies in that device's column of tiles of 512 x 512 cells. Of the live patterns of one device, at most 2 lie in any one row of tiles; in every column of tiles some row of tiles holds exactly 2 live patterns from every device of that column. The live patterns of device d are its first counts[d] slots; some device has 8.
All inputs are finite; a program needn't handle non-finite values.
Results may differ from a plain program's by a relative error of at most 0.0085.
The roundings to bfloat16 on the way count: a program that leaves them out, or rounds other values in their place, can miss the bound.
Values may be sent and summed in bfloat16 or wider, within the bound.
No kernel may reach another device: no remote copies, remote signals or barrier semaphores. Data moves between devices by JAX's collectives and lax.ppermute only.
A program may use at most 128 MiB of HBM per device.

v0:
```python
import math
import jax
import jax.numpy as jnp
from jax import lax
from jax.sharding import PartitionSpec as P

CAP = 2
PROPAGATION = 0.37


def extended_2(block, sides, width):
    for axis, dim in sides:
        count = lax.axis_size(axis)
        forward = [(i, i + 1) for i in range(count - 1)]
        backward = [(target, source) for source, target in forward]
        low = lax.ppermute(
            lax.slice_in_dim(block, block.shape[dim] - width, None, axis=dim), axis, forward
        )
        high = lax.ppermute(lax.slice_in_dim(block, 0, width, axis=dim), axis, backward)
        block = jnp.concatenate([low, block, high], axis=dim)
    return block


def make_tables(extent):
    indices = jnp.arange(extent, dtype=jnp.int32)
    product = indices[:, None] * indices[None, :] % extent
    angles = 2.0 * jnp.pi / extent * product.astype(jnp.float32)
    norm_scale = 1.0 / math.sqrt(extent)
    real_table = (jnp.cos(angles) * norm_scale).astype(jnp.bfloat16)
    imag_table = (-jnp.sin(angles) * norm_scale).astype(jnp.bfloat16)
    right_fwd = jnp.concatenate(
        [
            jnp.concatenate([real_table, imag_table], 1),
            jnp.concatenate([-imag_table, real_table], 1),
        ],
        0,
    )
    right_inv = jnp.concatenate(
        [
            jnp.concatenate([real_table, -imag_table], 1),
            jnp.concatenate([imag_table, real_table], 1),
        ],
        0,
    )
    left_fwd = jnp.concatenate([real_table, imag_table], 0)
    left_inv = jnp.concatenate([real_table, -imag_table], 0)
    frequency = jnp.where(indices < extent // 2, indices, indices - extent).astype(jnp.float32)
    phases = -jnp.pi * PROPAGATION / extent * (frequency[:, None] ** 2 + frequency[None, :] ** 2)
    kernel = jnp.stack([jnp.cos(phases), jnp.sin(phases)])
    return (right_fwd, left_fwd, right_inv, left_inv, kernel)


def transform(wave_field, right_table, left_table):
    extent = wave_field.shape[-1]
    rounded = wave_field.astype(jnp.bfloat16)
    joined = jnp.concatenate([rounded[:, 0], rounded[:, 1]], axis=-1)
    partial_value = jnp.einsum(
        "bpk,kq->bpq", joined, right_table, preferred_element_type=jnp.float32
    ).astype(jnp.bfloat16)
    stacked = jnp.einsum(
        "ij,bjq->biq", left_table, partial_value, preferred_element_type=jnp.float32
    )
    real_part = stacked[:, :extent, :extent] - stacked[:, extent:, extent:]
    imag_part = stacked[:, extent:, :extent] + stacked[:, :extent, extent:]
    return jnp.stack([real_part, imag_part], axis=1)


def complex_product(former, latter):
    former_re = former[..., 0, :, :]
    former_im = former[..., 1, :, :]
    latter_re = latter[..., 0, :, :]
    latter_im = latter[..., 1, :, :]
    return jnp.stack(
        [
            former_re * latter_re - former_im * latter_im,
            former_re * latter_im + former_im * latter_re,
        ],
        axis=-3,
    )


def conjugate(values):
    return jnp.stack([values[..., 0, :, :], -values[..., 1, :, :]], axis=-3)


def pattern_terms(window, amplitude, live_flag, probe_modes, tables):
    right_fwd, left_fwd, right_inv, left_inv, kernel = tables
    slices = window.shape[0]
    inputs = [probe_modes]
    far_field = None
    for slice_index in range(slices):
        exit_wave = complex_product(inputs[slice_index], window[slice_index])
        if slice_index + 1 < slices:
            spread_wave = complex_product(kernel, transform(exit_wave, right_fwd, left_fwd))
            inputs.append(transform(spread_wave, right_inv, left_inv))
        else:
            far_field = transform(exit_wave, right_fwd, left_fwd)
    intensity = jnp.sum(far_field[:, 0] ** 2 + far_field[:, 1] ** 2, axis=0)
    factor = (1.0 - amplitude / jnp.sqrt(jnp.maximum(intensity, 0.25))) * live_flag
    residue = far_field * factor
    backward = transform(residue, right_inv, left_inv)
    slice_grads = [None] * slices
    for slice_index in reversed(range(slices)):
        slice_grads[slice_index] = jnp.sum(
            complex_product(conjugate(inputs[slice_index]), backward), axis=0
        )
        if slice_index > 0:
            inner_wave = transform(
                complex_product(conjugate(window[slice_index]), backward), right_fwd, left_fwd
            )
            backward = transform(
                complex_product(conjugate(kernel), inner_wave), right_inv, left_inv
            )
    probe_term = complex_product(conjugate(window[0]), backward)
    return (jnp.stack(slice_grads), probe_term)


def settle(centre, leading, trailing, axis, margin):
    length = centre.shape[axis]
    top_part = lax.slice_in_dim(centre, 0, margin, axis=axis) + leading
    middle_part = lax.slice_in_dim(centre, margin, length - margin, axis=axis)
    bottom_part = lax.slice_in_dim(centre, length - margin, length, axis=axis) + trailing
    return jnp.concatenate([top_part, middle_part, bottom_part], axis=axis)


def on_device(object_slices, probe_modes, patterns, positions, counts):
    slices = object_slices.shape[0]
    tile_cells = object_slices.shape[2]
    extent = probe_modes.shape[-1]
    margin = extent // 2
    per_device = patterns.shape[0]
    row_count = lax.axis_size("ty")
    column_count = lax.axis_size("tx")
    row_index = lax.axis_index("ty")
    column_index = lax.axis_index("tx")
    position_grid = positions.reshape(row_count, column_count, per_device, 2)
    column = lax.dynamic_index_in_dim(position_grid, column_index, axis=1, keepdims=False)
    count_grid = counts.reshape(row_count, column_count)
    column_counts = lax.dynamic_index_in_dim(count_grid, column_index, axis=1, keepdims=False)
    ordinal = jnp.arange(per_device, dtype=jnp.int32)
    is_live = ordinal[None, :] < column_counts[:, None]
    target = column[:, :, 0] // tile_cells
    earlier = ordinal[None, :] < ordinal[:, None]
    same_row = is_live[:, None, :] & (target[:, None, :] == target[:, :, None]) & earlier[None]
    row_rank = jnp.sum(same_row.astype(jnp.int32), axis=2)
    slot_count = row_count * CAP
    slot_ids = jnp.arange(slot_count, dtype=jnp.int32)
    own_live = lax.dynamic_index_in_dim(is_live, row_index, axis=0, keepdims=False)
    own_slot = lax.dynamic_index_in_dim(target * CAP + row_rank, row_index, axis=0, keepdims=False)
    choose = (own_live[None, :] & (own_slot[None, :] == slot_ids[:, None])).astype(jnp.bfloat16)
    outgoing = jnp.einsum(
        "sj,jab->sab", choose, patterns, preferred_element_type=jnp.float32
    ).astype(jnp.bfloat16)
    incoming = lax.all_to_all(outgoing, "ty", split_axis=0, concat_axis=0, tiled=True)
    rank_ids = jnp.arange(CAP, dtype=jnp.int32)
    matched = (
        is_live[:, None, :]
        & (target[:, None, :] == row_index)
        & (row_rank[:, None, :] == rank_ids[None, :, None])
    )
    slot_live = jnp.any(matched, axis=2).reshape(-1)
    chosen = matched.astype(jnp.int32)
    centre_row = jnp.sum(chosen * column[:, None, :, 0], axis=2).reshape(-1)
    centre_col = jnp.sum(chosen * column[:, None, :, 1], axis=2).reshape(-1)
    local_row = jnp.where(slot_live, centre_row - row_index * tile_cells, 0)
    local_col = jnp.where(slot_live, centre_col - column_index * tile_cells, 0)
    extended = extended_2(object_slices, (("ty", 2), ("tx", 3)), margin)
    tables = make_tables(extent)

    def visit_slot(running, element):
        gradient, probe_grad = running
        amplitude, row_start, col_start, live_flag = element
        corner = (jnp.int32(0), jnp.int32(0), row_start, col_start)
        window = lax.dynamic_slice(extended, corner, (slices, 2, extent, extent))
        slice_grads, probe_term = pattern_terms(
            window, amplitude.astype(jnp.float32), live_flag, probe_modes, tables
        )
        current = lax.dynamic_slice(gradient, corner, (slices, 2, extent, extent))
        gradient = lax.dynamic_update_slice(gradient, current + slice_grads, corner)
        return ((gradient, probe_grad + probe_term), None)

    span_cells = tile_cells + extent
    initial = (
        jnp.zeros((slices, 2, span_cells, span_cells), jnp.float32),
        jnp.zeros(probe_modes.shape, jnp.float32),
    )
    (gradient, probe_grad), unused = lax.scan(
        visit_slot, initial, (incoming, local_row, local_col, slot_live.astype(jnp.float32))
    )
    row_edges = jnp.concatenate([gradient[:, :, :margin], gradient[:, :, -margin:]], axis=2)
    row_halo = extended_2(row_edges, (("ty", 2),), margin)
    row_folded = settle(
        gradient[:, :, margin : margin + tile_cells],
        row_halo[:, :, :margin],
        row_halo[:, :, -margin:],
        2,
        margin,
    )
    col_edges = jnp.concatenate([row_folded[..., :margin], row_folded[..., -margin:]], axis=3)
    col_halo = extended_2(col_edges, (("tx", 3),), margin)
    folded = settle(
        row_folded[..., margin : margin + tile_cells],
        col_halo[..., :margin],
        col_halo[..., -margin:],
        3,
        margin,
    )
    probe_power = jnp.mean(jnp.sum(probe_modes**2, axis=(0, 1)))
    new_object = object_slices - folded / (probe_power + 1e-06)
    summed = lax.psum(probe_grad, ("ty", "tx"))
    spread = jnp.sqrt(jnp.mean(summed * summed) + 1e-06)
    new_probe = probe_modes - 0.5 * summed / spread
    return (new_object, new_probe)


def solution(mesh):
    return jax.shard_map(
        on_device,
        mesh=mesh,
        in_specs=(P(None, None, "ty", "tx"), P(), P(("ty", "tx"), None, None), P(), P()),
        out_specs=(P(None, None, "ty", "tx"), P()),
        check_vma=False,
    )
```

profile of v0, /device:TPU:0, one launch (start us, length us, event | category | flops | bytes accessed | tf_op | source)
XLA Modules:
  0.0 498.1 jit_solution(16212770416473145393)
XLA Ops:
  10.3 6.3 %all-to-all-start = ((bf16[8,128,128]{2,1,0:T(8,128)(2,1)}), bf16[8,128,128]{2,1,0:T(8,128)(2,1)}, u32[]{:S(2)}, u32[]{:S(2)}) async-start(bf16[8,128,128]{2,1,0:T(8,128)(2,1)} %copy.108), calls=%async_computation | async-start | bytes 524288 | tf_op jit(solution)/shard_map/all_to_all | solution.py:154
  18.0 4.0 collective-permute-start
  23.2 5.2 %copy.120 = f32[2,2,512,512]{2,3,1,0:T(8,128)} copy(f32[2,2,512,512]{3,2,1,0:T(8,128)} %param.7) | data formatting | bytes 8388608 | tf_op args[0]
  32.8 4.0 collective-permute-done.1
  47.4 5.9 %pad_maximum_fusion = f32[2,2,640,640]{2,3,1,0:T(8,128)} fusion(f32[2,2,640,64]{2,3,1,0:T(8,128)} %collective-permute-done.3, f32[2,2,64,512]{2,3,1,0:T(8,128)S(1)} %copy.106, f32[2,2,512,512]{2,3,1,0:T(8,128)} %copy.120, f32[2,2,64,512]{2,3,1,0:T(8,128)S(1)} %copy.104, f32[2,2,640,64]{2,3,1,0:T(8,128)} %collective-permute-done.2), kind=kLoop, calls=%fused_computation.110 | loop fusion | flops 6553600 | bytes 13107200 | tf_op jit(solution)/shard_map/concatenate | solution.py:20
  53.3 3.2 broadcast_in_dim.8
  56.5 217.4 %while.18 = (s32[]{:T(128)}, f32[2,2,640,640]{2,3,1,0:T(8,128)}, f32[4,2,128,128]{3,2,0,1:T(8,128)S(1)}, s32[8]{0:T(128)S(1)}, s32[8]{0:T(128)S(1)}, /*index=5*/...) while((s32[]{:T(128)}, f32[2,2,640,640]{2,3,1,0:T(8,128)}, ...), condition=%wide.region_8.9_spmd.clone.clone.clone.clone, body=%wide.region_4.8_spmd.clone.clone.clone.clone.sunk | while | flops 815677440 | bytes 33391468 | solution.py:187
  79.3 4.4 dynamic_update_slice.10
  106.5 4.2 dynamic_update_slice.10
  133.5 4.4 dynamic_update_slice.10
  160.7 4.4 dynamic_update_slice.10
  187.9 4.4 dynamic_update_slice.10
  215.1 4.3 dynamic_update_slice.10
  242.2 4.4 dynamic_update_slice.10
  269.4 4.4 dynamic_update_slice.10
  273.8 8.2 %copy.114 = f32[2,2,640,640]{3,2,1,0:T(8,128)} copy(f32[2,2,640,640]{2,3,1,0:T(8,128)} %get-tuple-element.206) | data formatting | bytes 13107200 | tf_op jit(solution)/shard_map/while | solution.py:187
  285.0 8.0 %collective-permute-done.4 = f32[2,2,64,640]{3,2,1,0:T(8,128)S(1)} collective-permute-done((f32[2,2,64,640]{3,2,1,0:T(8,128)S(1)}, f32[2,2,64,640]{3,2,1,0:T(8,128)S(1)}, u32[]{:S(2)}, u32[]{:S(2)}) %collective-permute-start.4) | collective-permute-done | bytes 655392 | tf_op jit(solution)/shard_map/ppermute | solution.py:16
  296.8 4.2 slice.281
  301.4 7.1 %collective-permute-done.5 = f32[2,2,64,640]{3,2,1,0:T(8,128)S(1)} collective-permute-done((f32[2,2,64,640]{3,2,1,0:T(8,128)}, f32[2,2,64,640]{3,2,1,0:T(8,128)S(1)}, u32[]{:S(2)}, u32[]{:S(2)}) %collective-permute-start.5) | collective-permute-done | bytes 655392 | tf_op jit(solution)/shard_map/ppermute | solution.py:19
  314.0 14.0 %collective-permute-start.6 = (f32[2,2,512,64]{2,3,1,0:T(8,128)}, f32[2,2,512,64]{2,3,1,0:T(8,128)}, u32[]{:S(2)}, u32[]{:S(2)}) collective-permute-start(f32[2,2,512,64]{2,3,1,0:T(8,128)} %pad_maximum_fusion.6), channel_id=1, source_target_pairs={{0,1},{1,2},{2,3},{3,4},{4,5},{5,6},{6,7},{8,9},{9,10},{10,11},{11... | collective-permute-start | bytes 1572872 | tf_op jit(solution)/shard_map/ppermute | solution.py:16
  333.0 136.7 %all-reduce.2.cloned.1.call-done = f32[4,2,128,128]{3,2,1,0:T(8,128)} async-done(((f32[4,2,128,128]{3,2,1,0:T(8,128)}), f32[4,2,128,128]{3,2,1,0:T(8,128)}) %all-reduce.2.cloned.1.call-update) | async-done | bytes 524304 | tf_op jit(solution)/shard_map/psum | solution.py:210
  475.4 3.9 pad_maximum_fusion.1
  483.1 3.0 fusion.85
  486.1 5.2 %copy.122 = f32[2,2,512,512]{3,2,1,0:T(8,128)} copy(f32[2,2,512,512]{2,3,1,0:T(8,128)} %fusion.85) | data formatting | bytes 8388608
  (395 shorter events, 196.0 us)
Async XLA Ops:
  10.3 43.0 %all-to-all-start = ((bf16[8,128,128]{2,1,0:T(8,128)(2,1)}), bf16[8,128,128]{2,1,0:T(8,128)(2,1)}, u32[]{:S(2)}, u32[]{:S(2)}) async-start(bf16[8,128,128]{2,1,0:T(8,128)(2,1)} %copy.108), calls=%async_computation | async-start | bytes 524288 | tf_op jit(solution)/shard_map/all_to_all | solution.py:154
  16.7 453.1 %all-reduce.2.cloned.1.call-start = ((), (), s32[]{:S(2)}) async-start(), calls=%async_computation.1 | async-start | bytes 1048576 | tf_op jit(solution)/shard_map/psum | solution.py:210
  18.0 14.5 %collective-permute-start = (f32[2,2,64,512]{3,2,1,0:T(8,128)S(1)}, f32[2,2,64,512]{3,2,1,0:T(8,128)S(1)}, u32[]{:S(2)}, u32[]{:S(2)}) collective-permute-start(f32[2,2,64,512]{3,2,1,0:T(8,128)S(1)} %get-tuple-element.545), channel_id=1, source_target_pairs={{0,8},{8,16},{16,24},{1,9},{9,17},{17,25},{2,10},{10,18},{18,26},{... | collective-permute-start | bytes 1572872 | tf_op jit(solution)/shard_map/ppermute | solution.py:16
  21.9 14.9 %collective-permute-start.1 = (f32[2,2,64,512]{3,2,1,0:T(8,128)S(1)}, f32[2,2,64,512]{3,2,1,0:T(8,128)S(1)}, u32[]{:S(2)}, u32[]{:S(2)}) collective-permute-start(f32[2,2,64,512]{3,2,1,0:T(8,128)S(1)} %get-tuple-element.546), channel_id=1, source_target_pairs={{8,0},{16,8},{24,16},{9,1},{17,9},{25,17},{10,2},{18,10},{26,18},{... | collective-permute-start | bytes 1572872 | tf_op jit(solution)/shard_map/ppermute | solution.py:19
  37.1 6.3 %copy-start.9 = (bf16[128,128]{1,0:T(8,128)(2,1)S(1)}, bf16[128,128]{1,0:T(8,128)(2,1)}, u32[]{:S(2)}) copy-start(bf16[128,128]{1,0:T(8,128)(2,1)} %copy-done.8) | copy-start | bytes 98308
  37.2 6.3 %copy-start.11 = (bf16[128,128]{1,0:T(8,128)(2,1)S(1)}, bf16[128,128]{1,0:T(8,128)(2,1)}, u32[]{:S(2)}) copy-start(bf16[128,128]{1,0:T(8,128)(2,1)} %copy-done.10) | copy-start | bytes 98308
  37.2 6.3 %copy-start.13 = (bf16[128,128]{1,0:T(8,128)(2,1)S(1)}, bf16[128,128]{1,0:T(8,128)(2,1)}, u32[]{:S(2)}) copy-start(bf16[128,128]{1,0:T(8,128)(2,1)} %copy-done.12) | copy-start | bytes 98308
  37.2 6.3 %copy-start.14 = (pred[4,2]{0,1:T(4,128)(4,1)S(1)}, pred[4,2]{0,1:T(4,128)(4,1)}, u32[]{:S(2)}) copy-start(pred[4,2]{0,1:T(4,128)(4,1)} %reduce_or.9) | copy-start | bytes 28
  37.2 6.3 %copy-start.5 = (f32[4,2,128,128]{3,2,1,0:T(8,128)S(1)}, f32[4,2,128,128]{3,2,1,0:T(8,128)}, u32[]{:S(2)}) copy-start(f32[4,2,128,128]{3,2,1,0:T(8,128)} %param.8) | copy-start | bytes 1572868
  40.0 6.6 %collective-permute-start.2 = (f32[2,2,640,64]{2,3,1,0:T(8,128)}, f32[2,2,640,64]{2,3,1,0:T(8,128)}, u32[]{:S(2)}, u32[]{:S(2)}) collective-permute-start(f32[2,2,640,64]{2,3,1,0:T(8,128)} %get-tuple-element.543), channel_id=1, source_target_pairs={{0,1},{1,2},{2,3},{3,4},{4,5},{5,6},{6,7},{8,9},{9,10},{10,11},{11... | collective-permute-start | bytes 1966088 | tf_op jit(solution)/shard_map/ppermute | solution.py:16
  42.1 5.2 %collective-permute-start.3 = (f32[2,2,640,64]{2,3,1,0:T(8,128)}, f32[2,2,640,64]{2,3,1,0:T(8,128)}, u32[]{:S(2)}, u32[]{:S(2)}) collective-permute-start(f32[2,2,640,64]{2,3,1,0:T(8,128)} %get-tuple-element.544), channel_id=1, source_target_pairs={{1,0},{2,1},{3,2},{4,3},{5,4},{6,5},{7,6},{9,8},{10,9},{11,10},{12... | collective-permute-start | bytes 1966088 | tf_op jit(solution)/shard_map/ppermute | solution.py:19
  53.3 3.2 copy-start.15
  75.3 2.3 copy-start.4
  102.5 2.3 copy-start.4
  183.9 2.3 copy-start.4
  265.5 2.3 copy-start.4
  283.1 9.9 %collective-permute-start.4 = (f32[2,2,64,640]{3,2,1,0:T(8,128)S(1)}, f32[2,2,64,640]{3,2,1,0:T(8,128)S(1)}, u32[]{:S(2)}, u32[]{:S(2)}) collective-permute-start(f32[2,2,64,640]{3,2,1,0:T(8,128)S(1)} %slice.455), channel_id=1, source_target_pairs={{0,8},{8,16},{16,24},{1,9},{9,17},{17,25},{2,10},{10,18},{18,26},{... | collective-permute-start | bytes 1966088 | tf_op jit(solution)/shard_map/ppermute | solution.py:16
  295.3 13.1 %collective-permute-start.5 = (f32[2,2,64,640]{3,2,1,0:T(8,128)}, f32[2,2,64,640]{3,2,1,0:T(8,128)S(1)}, u32[]{:S(2)}, u32[]{:S(2)}) collective-permute-start(f32[2,2,64,640]{3,2,1,0:T(8,128)} %get-tuple-element.542), channel_id=1, source_target_pairs={{8,0},{16,8},{24,16},{9,1},{17,9},{25,17},{10,2},{18,10},{26,18},{... | collective-permute-start | bytes 1966088 | tf_op jit(solution)/shard_map/ppermute | solution.py:19
  314.0 15.1 %collective-permute-start.6 = (f32[2,2,512,64]{2,3,1,0:T(8,128)}, f32[2,2,512,64]{2,3,1,0:T(8,128)}, u32[]{:S(2)}, u32[]{:S(2)}) collective-permute-start(f32[2,2,512,64]{2,3,1,0:T(8,128)} %pad_maximum_fusion.6), channel_id=1, source_target_pairs={{0,1},{1,2},{2,3},{3,4},{4,5},{5,6},{6,7},{8,9},{9,10},{10,11},{11... | collective-permute-start | bytes 1572872 | tf_op jit(solution)/shard_map/ppermute | solution.py:16
  328.9 143.3 %copy-start.6 = (f32[4,2,128,128]{3,2,1,0:T(8,128)S(1)}, f32[4,2,128,128]{3,2,1,0:T(8,128)}, u32[]{:S(2)}) copy-start(f32[4,2,128,128]{3,2,1,0:T(8,128)} %param.8) | copy-start | bytes 1572868
  331.7 147.9 %collective-permute-start.7 = (f32[2,2,512,64]{2,3,1,0:T(8,128)}, f32[2,2,512,64]{2,3,1,0:T(8,128)}, u32[]{:S(2)}, u32[]{:S(2)}) collective-permute-start(f32[2,2,512,64]{2,3,1,0:T(8,128)} %get-tuple-element.540), channel_id=1, source_target_pairs={{1,0},{2,1},{3,2},{4,3},{5,4},{6,5},{7,6},{9,8},{10,9},{11,10},{12... | collective-permute-start | bytes 1572872 | tf_op jit(solution)/shard_map/ppermute | solution.py:19
  479.6 3.5 copy-start.3
  479.6 3.5 copy-start.7
  483.1 8.2 %copy-start.1 = (bf16[8,128,128]{2,1,0:T(8,128)(2,1)S(1)}, bf16[8,128,128]{2,1,0:T(8,128)(2,1)}, u32[]{:S(2)}) copy-start(bf16[8,128,128]{2,1,0:T(8,128)(2,1)} %param.9) | copy-start | bytes 786436
  (9 other events, 15.4 us)
Sparse Core Ops, SparseCore 0:
  329.0 140.7 all-reduce.1
where the time goes:
time: 503 us; the launch traced here: 498 us
  waiting for transfers between devices  159 us (32%)
  local copies, waits for them, and re-layouts  119 us (24%)
  other arithmetic  88.5 us (18%)
  matrix products  49.7 us (10%)
  starting transfers between devices  33.7 us (7%)
  loops' own time  32.6 us (6%)
  between operations  15.8 us (3%)
    psum x1, waiting for transfers between devices, on_device(): summed = lax.psum(probe_grad, ('ty', 'tx'))  137 us
    dot_general x48, matrix products, transform(): jnp.einsum('ij,bjq->biq', left_table, partial_value, preferred_element_ty...  49.5 us
    dynamic_update_slice x8, local copies, waits for them, and re-layouts, visit_slot(): gradient = lax.dynamic_update_slice(gradient, current + slice_grads, corner)  34.9 us
    another operation x1, loops' own time, on_device(): lax.scan(visit_slot, initial, (incoming, local_row, local_col, slot_live....  32.6 us
    dynamic_slice x40, local copies, waits for them, and re-layouts, on_device(): lax.scan(visit_slot, initial, (incoming, local_row, local_col, slot_live....  26.4 us
    ppermute x4, starting transfers between devices, extended_2(): lax.ppermute(lax.slice_in_dim(block, block.shape[dim] - width, None, axis...  22 us
    squeeze x48, other arithmetic, transform(): joined = jnp.concatenate([rounded[:, 0], rounded[:, 1]], axis=-1)  20.9 us
    unnamed x33, local copies, waits for them, and re-layouts  12.9 us
  transfers between devices with their start and end apart: 10, of which 7 were waited for; matrix products, arithmetic and copies ran while one was open for 7% of the time, Pallas kernels for 0%

commit v1 on v0

--- a/solution.py
+++ b/solution.py
@@ -207,7 +207,8 @@
     )
     probe_power = jnp.mean(jnp.sum(probe_modes**2, axis=(0, 1)))
     new_object = object_slices - folded / (probe_power + 1e-06)
-    summed = lax.psum(probe_grad, ("ty", "tx"))
+    terms = lax.all_gather(probe_grad, ("ty", "tx"))
+    summed = jnp.sum(terms, axis=0)
     spread = jnp.sqrt(jnp.mean(summed * summed) + 1e-06)
     new_probe = probe_modes - 0.5 * summed / spread
     return (new_object, new_probe)

time: 503 us -> 464 us (0.922)
  waiting for transfers between devices: 159 us -> 96.8 us
  other arithmetic: 88.5 us -> 104 us
  starting transfers between devices: 33.7 us -> 40.1 us
  local copies, waits for them, and re-layouts: 119 us -> 113 us
  matrix products: 49.7 us -> 55.2 us
    psum x1 -> x0, waiting for transfers between devices: 137 us -> none  [on_device(): summed = lax.psum(probe_grad, ('ty', 'tx'))]
    ppermute x4, waiting for transfers between devices: 11.7 us -> 57.6 us  [extended_2(): lax.ppermute(lax.slice_in_dim(block, 0, width, axis=dim), axis, backward)]
    all_gather x0 -> x1, waiting for transfers between devices: none -> 29.7 us  [on_device(): terms = lax.all_gather(probe_grad, ('ty', 'tx'))]
    another operation x24, other arithmetic: 2.18 us -> 16.5 us  [complex_product(): jnp.stack([former_re * latter_re - former_im * latter_im, former_re * lat...]
    squeeze x48, other arithmetic: 20.9 us -> 10.3 us  [transform(): joined = jnp.concatenate([rounded[:, 0], rounded[:, 1]], axis=-1)]
    ppermute x4, starting transfers between devices: 22 us -> 30.5 us  [extended_2(): lax.ppermute(lax.slice_in_dim(block, block.shape[dim] - width, None, axis...]
    reduce_sum x0 -> x2, other arithmetic: none -> 7.68 us  [the longest x1 6.98 us: on_device(): summed = jnp.sum(terms, axis=0)]
    neg x17, other arithmetic: 0.84 us -> 7.54 us  [conjugate(): return jnp.stack([values[..., 0, :, :], -values[..., 1, :, :]], axis=-3)]
  transfers between devices with their start and end apart: 10 -> 10, of which waited for: 7 -> 5; matrix products, arithmetic and copies ran while one was open for 7% -> 12% of each run, Pallas kernels for 0% -> 0%
where the time goes in v1:
time: 464 us; the launch traced here: 458 us
  local copies, waits for them, and re-layouts  113 us (24%)
  other arithmetic  104 us (22%)
  waiting for transfers between devices  96.8 us (21%)
  matrix products  55.2 us (12%)
  starting transfers between devices  40.1 us (9%)
  loops' own time  33.2 us (7%)
  between operations  15.7 us (3%)
    ppermute x4, waiting for transfers between devices, extended_2(): lax.ppermute(lax.slice_in_dim(block, 0, width, axis=dim), axis, backward)  57.6 us
    dot_general x48, matrix products, transform(): jnp.einsum('ij,bjq->biq', left_table, partial_value, preferred_element_ty...  54.9 us
    dynamic_update_slice x8, local copies, waits for them, and re-layouts, visit_slot(): gradient = lax.dynamic_update_slice(gradient, current + slice_grads, corner)  34.8 us
    another operation x1, loops' own time, on_device(): lax.scan(visit_slot, initial, (incoming, local_row, local_col, slot_live....  33.2 us
    ppermute x4, starting transfers between devices, extended_2(): lax.ppermute(lax.slice_in_dim(block, block.shape[dim] - width, None, axis...  30.5 us
    all_gather x1, waiting for transfers between devices, on_device(): terms = lax.all_gather(probe_grad, ('ty', 'tx'))  29.7 us
    dynamic_slice x40, local copies, waits for them, and re-layouts, on_device(): lax.scan(visit_slot, initial, (incoming, local_row, local_col, slot_live....  21.2 us
    another operation x24, other arithmetic, complex_product(): jnp.stack([former_re * latter_re - former_im * latter_im, former_re * lat...  16.5 us
  transfers between devices with their start and end apart: 10, of which 5 were waited for; matrix products, arithmetic and copies ran while one was open for 12% of the time, Pallas kernels for 0%

profile of v1, /device:TPU:0, one launch (start us, length us, event | category | flops | bytes accessed | tf_op | source)
XLA Modules:
  0.0 457.9 jit_solution(11382662136670310907)
XLA Ops:
  9.8 5.6 %collective-permute-start = (f32[2,2,64,512]{3,2,1,0:T(8,128)S(1)}, f32[2,2,64,512]{3,2,1,0:T(8,128)S(1)}, u32[]{:S(2)}, u32[]{:S(2)}) collective-permute-start(f32[2,2,64,512]{3,2,1,0:T(8,128)S(1)} %get-tuple-element.545), channel_id=1, source_target_pairs={{0,8},{8,16},{16,24},{1,9},{9,17},{17,25},{2,10},{10,18},{18,26},{... | collective-permute-start | bytes 1572872 | tf_op jit(solution)/shard_map/ppermute | solution.py:16
  18.6 4.3 all-to-all-start
  22.9 5.2 %copy.122 = f32[2,2,512,512]{2,3,1,0:T(8,128)} copy(f32[2,2,512,512]{3,2,1,0:T(8,128)} %param.7) | data formatting | bytes 8388608 | tf_op args[0]
  34.1 3.9 collective-permute-start.2
  41.1 6.1 %pad_maximum_fusion = f32[2,2,640,640]{2,3,1,0:T(8,128)} fusion(f32[2,2,640,64]{2,3,1,0:T(8,128)} %collective-permute-done.3, f32[2,2,64,512]{2,3,1,0:T(8,128)S(1)} %copy.108, f32[2,2,512,512]{2,3,1,0:T(8,128)} %copy.122, f32[2,2,64,512]{2,3,1,0:T(8,128)} %copy-done.11, f32[2,2,640,64]{2,3,1,0:T(8,128)} %collective-permute-done.2), kind=kLoop, calls=%fused_computation.110 | loop fusion | flops 6553600 | bytes 13107200 | tf_op jit(solution)/shard_map/concatenate | solution.py:20
  50.3 233.9 %while.18 = (s32[]{:T(128)}, f32[2,2,640,640]{2,3,1,0:T(8,128)}, f32[4,2,128,128]{3,2,0,1:T(8,128)S(1)}, s32[8]{0:T(128)S(1)}, s32[8]{0:T(128)S(1)}, /*index=5*/...) while((s32[]{:T(128)}, f32[2,2,640,640]{2,3,1,0:T(8,128)}, ...), condition=%wide.region_8.9_spmd.clone.clone.clone.clone, body=%wide.region_4.8_spmd.clone.clone.clone.clone.sunk | while | flops 815677440 | bytes 33915896 | solution.py:187
  75.1 4.3 dynamic_update_slice.10
  104.4 4.2 dynamic_update_slice.10
  133.5 4.4 dynamic_update_slice.10
  162.7 4.4 dynamic_update_slice.10
  192.0 4.4 dynamic_update_slice.10
  221.2 4.3 dynamic_update_slice.10
  250.5 4.4 dynamic_update_slice.10
  279.7 4.4 dynamic_update_slice.10
  285.0 8.2 %copy.116 = f32[2,2,640,640]{3,2,1,0:T(8,128)} copy(f32[2,2,640,640]{2,3,1,0:T(8,128)} %get-tuple-element.206) | data formatting | bytes 13107200 | tf_op jit(solution)/shard_map/while | solution.py:187
  296.7 8.0 %collective-permute-done.4 = f32[2,2,64,640]{3,2,1,0:T(8,128)S(1)} collective-permute-done((f32[2,2,64,640]{3,2,1,0:T(8,128)S(1)}, f32[2,2,64,640]{3,2,1,0:T(8,128)S(1)}, u32[]{:S(2)}, u32[]{:S(2)}) %collective-permute-start.4) | collective-permute-done | bytes 655392 | tf_op jit(solution)/shard_map/ppermute | solution.py:16
  307.8 4.3 slice.281
  312.4 15.2 %collective-permute-done.5 = f32[2,2,64,640]{3,2,1,0:T(8,128)S(1)} collective-permute-done((f32[2,2,64,640]{3,2,1,0:T(8,128)S(1)}, f32[2,2,64,640]{3,2,1,0:T(8,128)S(1)}, u32[]{:S(2)}, u32[]{:S(2)}) %collective-permute-start.5) | collective-permute-done | bytes 655392 | tf_op jit(solution)/shard_map/ppermute | solution.py:19
  330.6 18.5 %collective-permute-start.6 = (f32[2,2,512,64]{2,3,1,0:T(8,128)S(1)}, f32[2,2,512,64]{2,3,1,0:T(8,128)S(1)}, u32[]{:S(2)}, u32[]{:S(2)}) collective-permute-start(f32[2,2,512,64]{2,3,1,0:T(8,128)S(1)} %pad_maximum_fusion.6), channel_id=1, source_target_pairs={{0,1},{1,2},{2,3},{3,4},{4,5},{5,6},{6,7},{8,9},{9,10},{10,11},{11... | collective-permute-start | bytes 1572872 | tf_op jit(solution)/shard_map/ppermute | solution.py:16
  355.5 3.9 pad_maximum_fusion.1
  359.8 42.4 %collective-permute-done.7 = f32[2,2,512,64]{2,3,1,0:T(8,128)} collective-permute-done((f32[2,2,512,64]{2,3,1,0:T(8,128)}, f32[2,2,512,64]{2,3,1,0:T(8,128)}, u32[]{:S(2)}, u32[]{:S(2)}) %collective-permute-start.7) | collective-permute-done | bytes 524320 | tf_op jit(solution)/shard_map/ppermute | solution.py:19
  406.5 5.2 %copy.125 = f32[2,2,512,512]{3,2,1,0:T(8,128)} copy(f32[2,2,512,512]{2,3,1,0:T(8,128)} %fusion.85) | data formatting | bytes 8388608
  411.7 29.7 %all-gather.3.cloned.1.call-done = f32[128,2,128,128]{3,2,0,1:T(8,128)} async-done(((f32[4,2,128,128]{3,2,0,1:T(8,128)}), f32[128,2,128,128]{3,2,0,1:T(8,128)}) %all-gather.3.cloned.1.call-update) | async-done | bytes 16777232 | tf_op jit(solution)/shard_map/all_gather | solution.py:210
  441.3 7.0 %reduce_sum.95 = f32[4,2,128,128]{3,2,0,1:T(8,128)S(1)} reduce(f32[32,4,2,128,128]{4,3,1,0,2:T(8,128)} %bitcast.205, f32[]{:T(128)} %constant.97.clone.1), dimensions={0}, to_apply=%region_10.11 | reduce | flops 4063232 | bytes 17301508 | tf_op jit(solution)/shard_map/reduce_sum | solution.py:211
  (471 shorter events, 206.8 us)
Async XLA Ops:
  7.2 10.4 %copy-start = (bf16[8,128,128]{2,1,0:T(8,128)(2,1)S(1)}, bf16[8,128,128]{2,1,0:T(8,128)(2,1)}, u32[]{:S(2)}) copy-start(bf16[8,128,128]{2,1,0:T(8,128)(2,1)} %param.9) | copy-start | bytes 786436
  8.5 20.4 %collective-permute-start.1 = (f32[2,2,64,512]{3,2,1,0:T(8,128)S(1)}, f32[2,2,64,512]{3,2,1,0:T(8,128)S(1)}, u32[]{:S(2)}, u32[]{:S(2)}) collective-permute-start(f32[2,2,64,512]{3,2,1,0:T(8,128)S(1)} %get-tuple-element.546), channel_id=1, source_target_pairs={{8,0},{16,8},{24,16},{9,1},{17,9},{25,17},{10,2},{18,10},{26,18},{... | collective-permute-start | bytes 1572872 | tf_op jit(solution)/shard_map/ppermute | solution.py:19
  9.8 19.5 %collective-permute-start = (f32[2,2,64,512]{3,2,1,0:T(8,128)S(1)}, f32[2,2,64,512]{3,2,1,0:T(8,128)S(1)}, u32[]{:S(2)}, u32[]{:S(2)}) collective-permute-start(f32[2,2,64,512]{3,2,1,0:T(8,128)S(1)} %get-tuple-element.545), channel_id=1, source_target_pairs={{0,8},{8,16},{16,24},{1,9},{9,17},{17,25},{2,10},{10,18},{18,26},{... | collective-permute-start | bytes 1572872 | tf_op jit(solution)/shard_map/ppermute | solution.py:16
  18.6 28.6 %all-to-all-start = ((bf16[8,128,128]{2,1,0:T(8,128)(2,1)}), bf16[8,128,128]{2,1,0:T(8,128)(2,1)}, u32[]{:S(2)}, u32[]{:S(2)}) async-start(bf16[8,128,128]{2,1,0:T(8,128)(2,1)} %copy.110), calls=%async_computation | async-start | bytes 524288 | tf_op jit(solution)/shard_map/all_to_all | solution.py:154
  22.9 418.5 %all-gather.3.cloned.1.call-start = ((), (), s32[]{:S(2)}) async-start(), calls=%async_computation.1 | async-start | bytes 17301504 | tf_op jit(solution)/shard_map/all_gather | solution.py:210
  32.8 8.2 %collective-permute-start.3 = (f32[2,2,640,64]{2,3,1,0:T(8,128)}, f32[2,2,640,64]{2,3,1,0:T(8,128)}, u32[]{:S(2)}, u32[]{:S(2)}) collective-permute-start(f32[2,2,640,64]{2,3,1,0:T(8,128)} %get-tuple-element.544), channel_id=1, source_target_pairs={{1,0},{2,1},{3,2},{4,3},{5,4},{6,5},{7,6},{9,8},{10,9},{11,10},{12... | collective-permute-start | bytes 1966088 | tf_op jit(solution)/shard_map/ppermute | solution.py:19
  34.1 6.9 %collective-permute-start.2 = (f32[2,2,640,64]{2,3,1,0:T(8,128)}, f32[2,2,640,64]{2,3,1,0:T(8,128)}, u32[]{:S(2)}, u32[]{:S(2)}) collective-permute-start(f32[2,2,640,64]{2,3,1,0:T(8,128)} %get-tuple-element.543), channel_id=1, source_target_pairs={{0,1},{1,2},{2,3},{3,4},{4,5},{5,6},{6,7},{8,9},{9,10},{10,11},{11... | collective-permute-start | bytes 1966088 | tf_op jit(solution)/shard_map/ppermute | solution.py:16
  50.3 10.7 %copy-start.6 = (bf16[256,128]{1,0:T(8,128)(2,1)}, bf16[256,128]{1,0:T(8,128)(2,1)S(1)}, u32[]{:S(2)}) copy-start(bf16[256,128]{1,0:T(8,128)(2,1)S(1)} %get-tuple-element.766) | copy-start | bytes 196612 | tf_op jit(solution)/shard_map/while
  79.5 10.7 %copy-start.6 = (bf16[256,128]{1,0:T(8,128)(2,1)}, bf16[256,128]{1,0:T(8,128)(2,1)S(1)}, u32[]{:S(2)}) copy-start(bf16[256,128]{1,0:T(8,128)(2,1)S(1)} %get-tuple-element.766) | copy-start | bytes 196612 | tf_op jit(solution)/shard_map/while
  108.6 10.7 %copy-start.6 = (bf16[256,128]{1,0:T(8,128)(2,1)}, bf16[256,128]{1,0:T(8,128)(2,1)S(1)}, u32[]{:S(2)}) copy-start(bf16[256,128]{1,0:T(8,128)(2,1)S(1)} %get-tuple-element.766) | copy-start | bytes 196612 | tf_op jit(solution)/shard_map/while
  137.9 10.7 %copy-start.6 = (bf16[256,128]{1,0:T(8,128)(2,1)}, bf16[256,128]{1,0:T(8,128)(2,1)S(1)}, u32[]{:S(2)}) copy-start(bf16[256,128]{1,0:T(8,128)(2,1)S(1)} %get-tuple-element.766) | copy-start | bytes 196612 | tf_op jit(solution)/shard_map/while
  167.1 10.7 %copy-start.6 = (bf16[256,128]{1,0:T(8,128)(2,1)}, bf16[256,128]{1,0:T(8,128)(2,1)S(1)}, u32[]{:S(2)}) copy-start(bf16[256,128]{1,0:T(8,128)(2,1)S(1)} %get-tuple-element.766) | copy-start | bytes 196612 | tf_op jit(solution)/shard_map/while
  196.4 10.7 %copy-start.6 = (bf16[256,128]{1,0:T(8,128)(2,1)}, bf16[256,128]{1,0:T(8,128)(2,1)S(1)}, u32[]{:S(2)}) copy-start(bf16[256,128]{1,0:T(8,128)(2,1)S(1)} %get-tuple-element.766) | copy-start | bytes 196612 | tf_op jit(solution)/shard_map/while
  225.6 10.7 %copy-start.6 = (bf16[256,128]{1,0:T(8,128)(2,1)}, bf16[256,128]{1,0:T(8,128)(2,1)S(1)}, u32[]{:S(2)}) copy-start(bf16[256,128]{1,0:T(8,128)(2,1)S(1)} %get-tuple-element.766) | copy-start | bytes 196612 | tf_op jit(solution)/shard_map/while
  254.8 10.7 %copy-start.6 = (bf16[256,128]{1,0:T(8,128)(2,1)}, bf16[256,128]{1,0:T(8,128)(2,1)S(1)}, u32[]{:S(2)}) copy-start(bf16[256,128]{1,0:T(8,128)(2,1)S(1)} %get-tuple-element.766) | copy-start | bytes 196612 | tf_op jit(solution)/shard_map/while
  294.3 10.5 %collective-permute-start.4 = (f32[2,2,64,640]{3,2,1,0:T(8,128)S(1)}, f32[2,2,64,640]{3,2,1,0:T(8,128)S(1)}, u32[]{:S(2)}, u32[]{:S(2)}) collective-permute-start(f32[2,2,64,640]{3,2,1,0:T(8,128)S(1)} %slice.455), channel_id=1, source_target_pairs={{0,8},{8,16},{16,24},{1,9},{9,17},{17,25},{2,10},{10,18},{18,26},{... | collective-permute-start | bytes 1966088 | tf_op jit(solution)/shard_map/ppermute | solution.py:16
  306.3 21.3 %collective-permute-start.5 = (f32[2,2,64,640]{3,2,1,0:T(8,128)S(1)}, f32[2,2,64,640]{3,2,1,0:T(8,128)S(1)}, u32[]{:S(2)}, u32[]{:S(2)}) collective-permute-start(f32[2,2,64,640]{3,2,1,0:T(8,128)S(1)} %get-tuple-element.542), channel_id=1, source_target_pairs={{8,0},{16,8},{24,16},{9,1},{17,9},{25,17},{10,2},{18,10},{26,18},{... | collective-permute-start | bytes 1966088 | tf_op jit(solution)/shard_map/ppermute | solution.py:19
  329.2 21.4 %copy-start.2 = (f32[2,2,384,640]{2,3,1,0:T(8,128)S(1)}, f32[2,2,384,640]{2,3,1,0:T(8,128)}, u32[]{:S(2)}) copy-start(f32[2,2,384,640]{2,3,1,0:T(8,128)} %slice.281) | copy-start | bytes 11796484
  330.6 22.7 %copy-start.14 = (f32[4,2,128,128]{3,2,1,0:T(8,128)S(1)}, f32[4,2,128,128]{3,2,1,0:T(8,128)}, u32[]{:S(2)}) copy-start(f32[4,2,128,128]{3,2,1,0:T(8,128)} %param.8) | copy-start | bytes 1572868
  330.6 20.0 %collective-permute-start.6 = (f32[2,2,512,64]{2,3,1,0:T(8,128)S(1)}, f32[2,2,512,64]{2,3,1,0:T(8,128)S(1)}, u32[]{:S(2)}, u32[]{:S(2)}) collective-permute-start(f32[2,2,512,64]{2,3,1,0:T(8,128)S(1)} %pad_maximum_fusion.6), channel_id=1, source_target_pairs={{0,1},{1,2},{2,3},{3,4},{4,5},{5,6},{6,7},{8,9},{9,10},{10,11},{11... | collective-permute-start | bytes 1572872 | tf_op jit(solution)/shard_map/ppermute | solution.py:16
  352.0 50.2 %collective-permute-start.7 = (f32[2,2,512,64]{2,3,1,0:T(8,128)}, f32[2,2,512,64]{2,3,1,0:T(8,128)}, u32[]{:S(2)}, u32[]{:S(2)}) collective-permute-start(f32[2,2,512,64]{2,3,1,0:T(8,128)} %get-tuple-element.540), channel_id=1, source_target_pairs={{1,0},{2,1},{3,2},{4,3},{5,4},{6,5},{7,6},{9,8},{10,9},{11,10},{12... | collective-permute-start | bytes 1572872 | tf_op jit(solution)/shard_map/ppermute | solution.py:19
  359.4 42.8 %copy-start.3 = (f32[2,2,384,640]{2,3,1,0:T(8,128)S(1)}, f32[2,2,384,640]{2,3,1,0:T(8,128)}, u32[]{:S(2)}) copy-start(f32[2,2,384,640]{2,3,1,0:T(8,128)} %slice.281) | copy-start | bytes 11796484
  359.7 43.8 %copy-start.4 = (f32[2,2,512,512]{2,3,1,0:T(8,128)S(1)}, f32[2,2,512,512]{2,3,1,0:T(8,128)}, u32[]{:S(2)}) copy-start(f32[2,2,512,512]{2,3,1,0:T(8,128)} %copy.122) | copy-start | bytes 12582916
  359.7 43.8 %copy-start.15 = (f32[2,2,512,64]{2,3,1,0:T(8,128)S(1)}, f32[2,2,512,64]{2,3,1,0:T(8,128)}, u32[]{:S(2)}) copy-start(f32[2,2,512,64]{2,3,1,0:T(8,128)} %get-tuple-element.539) | copy-start | bytes 1572868
  (45 other events, 195.1 us)
Sparse Core Ops, SparseCore 0:
  285.1 156.2 all-gather.2
